TPU v7x, 32 devices: a whole 2x2x4 slice. The times are simulated.
32 devices in a mesh: dim: 8 (over y, x, core), batch: 4 (over z).
Axes of the slice: x: 2, y: 2, z: 4, core: 2. Of those that a mesh axis runs over, the one named last changes fastest.
Arguments:
- start: float32 [1024, 4096], P('batch', 'dim'), may hold values from -6 to 6
- increments: float32 [3, 1024, 4096], P(None, 'batch', 'dim'), may hold values from -0.75 to 0.75
- w_in: bfloat16 [4096, 4096], P(None, 'dim'), may hold values from -0.09375 to 0.09375
- w_out: bfloat16 [4096, 4096], P('dim'), may hold values from -0.09375 to 0.09375
- initial: float32 [], replicated, may hold values from 4 to 5.5
Outputs:
- residual: float32 [1024], P('batch')
- grad_in: float32 [4096, 4096], P('batch', 'dim')
- grad_out: float32 [4096, 4096], P('dim', 'batch')
All inputs are finite; a program needn't handle non-finite values.
Results may differ from a plain program's by a relative error of at most 0.0051.
Values may be sent and summed in bfloat16 or wider, within the bound.
No kernel may reach another device: no remote copies, remote signals or barrier semaphores. Data moves between devices by JAX's collectives and lax.ppermute only.
A program may use at most 128 MiB of HBM per device.

v0:
```python
import math
import jax
import jax.numpy as jnp
from jax import lax
from jax.sharding import PartitionSpec as P

D = 4096
STEPS = 3
time_step = 1.0 / 64.0
lam_coef = 50.0
noise_coef = math.sqrt(2.0)


def on_device(start, increments, w_in, w_out, initial):
    zscale = 2.0 / math.sqrt(D)
    state = start
    saved = []
    ysum = jnp.zeros((start.shape[0],), jnp.float32)
    out_cols = lax.all_to_all(w_out, "dim", split_axis=1, concat_axis=0, tiled=True)
    for step in range(STEPS):
        inc = increments[step]
        whole = lax.all_gather(state.astype(jnp.bfloat16), "dim", axis=1, tiled=True)
        hidden = jnp.dot(whole, w_in, preferred_element_type=jnp.float32)
        act = jax.nn.silu(hidden).astype(jnp.bfloat16)
        act_whole = lax.all_gather(act, "dim", axis=1, tiled=True)
        zval = zscale * jnp.dot(act_whole, out_cols, preferred_element_type=jnp.float32)
        inner = jnp.sum(zval * inc, 1)
        square = jnp.sum(zval * zval, 1)
        inner_all, square_all = lax.psum((inner, square), "dim")
        ysum = ysum + 0.5 * lam_coef * time_step * square_all + inner_all
        saved.append((whole, hidden, act, zval))
        state = state + noise_coef * inc
    norm_local = jnp.sum(state * state, 1)
    norm_sq = lax.psum(norm_local, "dim")
    residual = initial + ysum - jnp.log((1.0 + norm_sq) * 0.5)
    grad_in = jnp.zeros(w_in.shape, jnp.float32)
    grad_out = jnp.zeros(w_out.shape, jnp.float32)
    reduced_in = None
    reduced_out = None
    for step in range(STEPS):
        whole, hidden, act, zval = saved[step]
        gz = (zscale * residual[:, None] * (lam_coef * time_step * zval + increments[step])).astype(
            jnp.bfloat16
        )
        gz_whole = lax.all_gather(gz, "dim", axis=1, tiled=True)
        term_out = jnp.dot(act.T, gz_whole, preferred_element_type=jnp.float32)
        ga = jnp.dot(gz_whole, w_out.T, preferred_element_type=jnp.float32)
        sig = jax.nn.sigmoid(hidden)
        gh = (ga * sig * (1.0 + hidden * (1.0 - sig))).astype(jnp.bfloat16)
        term_in = jnp.dot(whole.T, gh, preferred_element_type=jnp.float32)
        grad_in = grad_in + term_in
        grad_out = grad_out + term_out
    reduced_in, reduced_out = (
        lax.psum_scatter(grad_in, "batch", scatter_dimension=0, tiled=True),
        lax.psum_scatter(grad_out, "batch", scatter_dimension=1, tiled=True),
    )
    return (residual, reduced_in, reduced_out)


def solution(mesh):
    return jax.shard_map(
        on_device,
        mesh=mesh,
        in_specs=(P("batch", "dim"), P(None, "batch", "dim"), P(None, "dim"), P("dim", None), P()),
        out_specs=(P("batch"), P("batch", "dim"), P("dim", "batch")),
        check_vma=False,
    )
```

profile of v0, /device:TPU:0, one launch (start us, length us, event | category | flops | bytes accessed | tf_op | source)
XLA Modules:
  0.0 635.2 jit_solution(16171568415561256104)
XLA Ops:
  7.2 0.0 all-gather.18.cloned.1.call-start
  7.2 2.6 fusion.35
  9.8 0.0 all-gather.18.cloned.1.call-update
  9.9 0.0 all-gather.14.cloned.1.call-start
  9.9 0.7 all-gather.14.cloned.1.call-update
  10.6 0.0 all-gather.10.cloned.1.call-start
  10.7 0.7 all-gather.10.cloned.1.call-update
  11.4 0.0 all-gather.20.cloned.1.call-start
  11.4 29.9 %all-gather.18.cloned.1.call-done = bf16[256,4096]{1,0:T(8,128)(2,1)} async-done(((bf16[256,512]{1,0:T(8,128)(2,1)}), bf16[256,4096]{1,0:T(8,128)(2,1)}) %all-gather.18.cloned.1.call-update) | async-done | bytes 2097168 | tf_op jit(solution)/shard_map/all_gather | solution.py:22
  41.3 4.9 multiply_convert_fusion
  46.1 0.0 all-gather.20.cloned.1.call-update
  46.2 0.0 all-gather.16.cloned.1.call-start
  46.2 25.6 %all-gather.14.cloned.1.call-done = bf16[256,4096]{1,0:T(8,128)(2,1)} async-done(((bf16[256,512]{1,0:T(8,128)(2,1)}), bf16[256,4096]{1,0:T(8,128)(2,1)}) %all-gather.14.cloned.1.call-update) | async-done | bytes 2097168 | tf_op jit(solution)/shard_map/all_gather | solution.py:22
  71.9 4.9 multiply_convert_fusion.1
  76.7 0.0 all-gather.16.cloned.1.call-update
  76.8 6.5 %copy.14 = bf16[512,4096]{0,1:T(8,128)(2,1)} copy(bf16[512,4096]{1,0:T(8,128)(2,1)} %param.8) | data formatting | bytes 8388608 | tf_op args[3]
  83.3 4.6 all-to-all-start
  87.9 0.0 all-gather.12.cloned.1.call-start
  87.9 19.7 %all-gather.10.cloned.1.call-done = bf16[256,4096]{1,0:T(8,128)(2,1)} async-done(((bf16[256,512]{1,0:T(8,128)(2,1)}), bf16[256,4096]{1,0:T(8,128)(2,1)}) %all-gather.10.cloned.1.call-update) | async-done | bytes 2097168 | tf_op jit(solution)/shard_map/all_gather | solution.py:22
  107.6 5.0 multiply_convert_fusion.2
  112.6 0.0 all-gather.12.cloned.1.call-update
  112.6 0.0 all-gather.22.cloned.1.call-start
  113.3 33.4 %all-to-all-done = bf16[512,8,512]{0,2,1:T(8,128)(2,1)} async-done(((bf16[512,8,512]{0,2,1:T(8,128)(2,1)}), bf16[512,8,512]{0,2,1:T(8,128)(2,1)}, u32[]{:S(2)}, u32[]{:S(2)}) %all-to-all-start) | async-done | bytes 4194336 | tf_op jit(solution)/shard_map/all_to_all | solution.py:19
  146.7 6.6 %copy.15 = bf16[8,512,512]{2,1,0:T(8,128)(2,1)} copy(bf16[8,512,512]{1,2,0:T(8,128)(2,1)} %bitcast.1) | data formatting | bytes 8388608 | tf_op jit(solution)/shard_map/all_to_all | solution.py:19
  153.3 0.0 all-gather.20.cloned.1.call-done
  153.3 4.1 fusion.41
  157.3 0.0 copy-start.4
  157.3 24.5 %all-gather.16.cloned.1.call-done = bf16[256,4096]{1,0:T(8,128)(2,1)} async-done(((bf16[256,512]{1,0:T(8,128)(2,1)}), bf16[256,4096]{1,0:T(8,128)(2,1)}) %all-gather.16.cloned.1.call-update) | async-done | bytes 2097168 | tf_op jit(solution)/shard_map/all_gather | solution.py:25
  181.8 4.9 fusion.40
  186.7 25.0 %all-gather.12.cloned.1.call-done = bf16[256,4096]{1,0:T(8,128)(2,1)} async-done(((bf16[256,512]{1,0:T(8,128)(2,1)}), bf16[256,4096]{1,0:T(8,128)(2,1)}) %all-gather.12.cloned.1.call-update) | async-done | bytes 2097168 | tf_op jit(solution)/shard_map/all_gather | solution.py:25
  211.7 0.0 copy-done.4
  211.7 5.3 fusion.19
  217.0 13.3 %all-reduce = (f32[256]{0:T(256)S(1)}, f32[256]{0:T(256)S(1)}, f32[256]{0:T(256)S(1)}, f32[256]{0:T(256)S(1)}, f32[256]{0:T(256)S(1)}, /*index=5*/f32[256]{0:T(256)S(1)}, f32[256]{0:T(256)S(1)}) all-reduce(f32[256]{0:T(256)S(1)} %get-tuple-element.13, f32[256]{0:T(256)S(1)} %get-tuple-element.14, ...), channel_id=1, replica_groups=mesh['dim'=8,'batch'=4] {'dim'}, use_global_device_ids=true, to_apply=%region_13.14 | all-reduce | flops 1792 | bytes 14336 | tf_op jit(solution)/shard_map/psum | solution.py:34
  230.3 0.6 broadcast_multiply_fusion
  230.9 2.4 fusion.14
  233.2 0.0 all-gather.22.cloned.1.call-update
  233.3 0.0 all-gather.24.cloned.1.call-start
  233.3 0.7 all-gather.24.cloned.1.call-update
  234.0 0.0 all-gather.26.cloned.1.call-start
  234.1 0.7 all-gather.26.cloned.1.call-update
  234.7 0.2 reduce-scatter.3.cloned.1.call-start
  235.0 26.5 %all-gather.22.cloned.1.call-done = bf16[256,4096]{1,0:T(8,128)(2,1)} async-done(((bf16[256,512]{1,0:T(8,128)(2,1)}), bf16[256,4096]{1,0:T(8,128)(2,1)}) %all-gather.22.cloned.1.call-update) | async-done | bytes 2097168 | tf_op jit(solution)/shard_map/all_gather | solution.py:45
  261.5 9.6 %fusion.8 = f32[512,4096]{1,0:T(8,128)} fusion(bf16[256,4096]{1,0:T(8,128)(2,1)} %all-gather.10.cloned.1.call-done, bf16[256,4096]{1,0:T(8,128)(2,1)} %all-gather.22.cloned.1.call-done, bf16[512,4096]{1,0:T(8,128)(2,1)} %param.8, f32[256,512]{1,0:T(8,128)} %get-tuple-element.35), kind=kOutput, calls=%fused_computation.13 | convolution fusion | flops 2148663296 | bytes 17301504 | tf_op jit(solution)/shard_map/dot_general | solution.py:50
  271.1 20.4 %all-gather.24.cloned.1.call-done = bf16[256,4096]{1,0:T(8,128)(2,1)} async-done(((bf16[256,512]{1,0:T(8,128)(2,1)}), bf16[256,4096]{1,0:T(8,128)(2,1)}) %all-gather.24.cloned.1.call-update) | async-done | bytes 2097168 | tf_op jit(solution)/shard_map/all_gather | solution.py:45
  291.5 0.0 copy-done.3
  291.5 8.7 %fusion.6 = f32[4096,512]{0,1:T(8,128)} fusion(bf16[256,4096]{1,0:T(8,128)(2,1)S(1)} %copy-done.3, bf16[256,4096]{1,0:T(8,128)(2,1)} %all-gather.24.cloned.1.call-done, bf16[512,4096]{1,0:T(8,128)(2,1)} %param.8, f32[256,512]{1,0:T(8,128)S(1)} %get-tuple-element.39), kind=kOutput, calls=%fused_computation.11 | convolution fusion | flops 2148663296 | bytes 17301504 | tf_op jit(solution)/shard_map/dot_general | solution.py:50
  300.2 21.4 %all-gather.26.cloned.1.call-done = bf16[256,4096]{1,0:T(8,128)(2,1)} async-done(((bf16[256,512]{1,0:T(8,128)(2,1)}), bf16[256,4096]{1,0:T(8,128)(2,1)}) %all-gather.26.cloned.1.call-update) | async-done | bytes 2097168 | tf_op jit(solution)/shard_map/all_gather | solution.py:45
  321.5 14.1 %fusion = f32[4096,512]{0,1:T(8,128)} fusion(f32[4096,512]{0,1:T(8,128)} %fusion.6, f32[512,4096]{1,0:T(8,128)} %fusion.8, bf16[256,4096]{1,0:T(8,128)(2,1)} %all-gather.18.cloned.1.call-done, bf16[256,4096]{1,0:T(8,128)(2,1)} %all-gather.26.cloned.1.call-done, bf16[512,4096]{1,0:T(8,128)(2,1)} %param.8, f32[256,512]{1,0:T(8,128)S(1)} %get-tuple-element.37), kind=kOutput, calls=%fused_computation.1 | convolution fusion | flops 2152857600 | bytes 34078720 | tf_op jit(solution)/shard_map/dot_general | solution.py:50
  335.6 0.0 reduce-scatter.3.cloned.1.call-update
  335.6 0.0 copy-start.6
  335.6 0.0 reduce-scatter.5.cloned.1.call-start
  335.7 1.5 copy-done
  337.2 0.0 copy-done.7
  337.2 1.3 fusion.42
  338.5 0.0 copy-done.6
  338.5 0.3 copy-done.1
  338.8 1.3 fusion.43
  340.1 0.3 copy-done.2
  340.4 0.0 copy-done.5
  340.4 4.6 add_add_fusion
  345.0 0.0 reduce-scatter.5.cloned.1.call-update
  345.0 135.4 %reduce-scatter.3.cloned.1.call-done = f32[1024,512]{0,1:T(8,128)} async-done(((f32[4096,512]{0,1:T(8,128)}), f32[1024,512]{0,1:T(8,128)}) %reduce-scatter.3.cloned.1.call-update) | async-done | bytes 2097168 | tf_op jit(solution)/shard_map/reduce_scatter | solution.py:54
  480.4 2.9 copy.18
  483.3 145.3 %reduce-scatter.5.cloned.1.call-done = f32[512,1024]{1,0:T(8,128)} async-done(((f32[512,4096]{1,0:T(8,128)}), f32[512,1024]{1,0:T(8,128)}) %reduce-scatter.5.cloned.1.call-update) | async-done | bytes 2097168 | tf_op jit(solution)/shard_map/reduce_scatter | solution.py:55
  (6 shorter events, 0.0 us)
Async XLA Ops:
  7.2 34.1 %all-gather.18.cloned.1.call-start = ((), (), s32[]{:S(2)}) async-start(), calls=%async_computation.7 | async-start | bytes 2359296 | tf_op jit(solution)/shard_map/all_gather | solution.py:22
  9.9 62.0 %all-gather.14.cloned.1.call-start = ((), (), s32[]{:S(2)}) async-start(), calls=%async_computation.5 | async-start | bytes 2359296 | tf_op jit(solution)/shard_map/all_gather | solution.py:22
  10.6 97.0 %all-gather.10.cloned.1.call-start = ((), (), s32[]{:S(2)}) async-start(), calls=%async_computation.3 | async-start | bytes 2359296 | tf_op jit(solution)/shard_map/all_gather | solution.py:22
  11.4 141.9 %all-gather.20.cloned.1.call-start = ((), (), s32[]{:S(2)}) async-start(), calls=%async_computation.8 | async-start | bytes 2359296 | tf_op jit(solution)/shard_map/all_gather | solution.py:25
  46.2 135.7 %all-gather.16.cloned.1.call-start = ((), (), s32[]{:S(2)}) async-start(), calls=%async_computation.6 | async-start | bytes 2359296 | tf_op jit(solution)/shard_map/all_gather | solution.py:25
  83.3 63.4 %all-to-all-start = ((bf16[512,8,512]{0,2,1:T(8,128)(2,1)}), bf16[512,8,512]{0,2,1:T(8,128)(2,1)}, u32[]{:S(2)}, u32[]{:S(2)}) async-start(bf16[512,8,512]{0,2,1:T(8,128)(2,1)} %bitcast.86), calls=%async_computation | async-start | bytes 8388608 | tf_op jit(solution)/shard_map/all_to_all | solution.py:19
  87.9 123.8 %all-gather.12.cloned.1.call-start = ((), (), s32[]{:S(2)}) async-start(), calls=%async_computation.4 | async-start | bytes 2359296 | tf_op jit(solution)/shard_map/all_gather | solution.py:25
  112.6 148.9 %all-gather.22.cloned.1.call-start = ((), (), s32[]{:S(2)}) async-start(), calls=%async_computation.9 | async-start | bytes 2359296 | tf_op jit(solution)/shard_map/all_gather | solution.py:45
  157.3 54.4 %copy-start.4 = (f32[3,256,512]{2,1,0:T(8,128)S(1)}, f32[3,256,512]{2,1,0:T(8,128)}, u32[]{:S(2)}) copy-start(f32[3,256,512]{2,1,0:T(8,128)} %param.6) | copy-start | bytes 4718596
  233.3 58.3 %all-gather.24.cloned.1.call-start = ((), (), s32[]{:S(2)}) async-start(), calls=%async_computation.10 | async-start | bytes 2359296 | tf_op jit(solution)/shard_map/all_gather | solution.py:45
  234.0 87.5 %all-gather.26.cloned.1.call-start = ((), (), s32[]{:S(2)}) async-start(), calls=%async_computation.11 | async-start | bytes 2359296 | tf_op jit(solution)/shard_map/all_gather | solution.py:45
  234.7 245.7 %reduce-scatter.3.cloned.1.call-start = ((), (), s32[]{:S(2)}) async-start(), calls=%async_computation.12 | async-start | bytes 10485760 | tf_op jit(solution)/shard_map/reduce_scatter | solution.py:54
  261.5 30.0 %copy-start.3 = (bf16[256,4096]{1,0:T(8,128)(2,1)S(1)}, bf16[256,4096]{1,0:T(8,128)(2,1)}, u32[]{:S(2)}) copy-start(bf16[256,4096]{1,0:T(8,128)(2,1)} %all-gather.14.cloned.1.call-done) | copy-start | bytes 6291460
  335.6 1.6 copy-start
  335.6 1.6 copy-start.7
  335.6 2.8 copy-start.6
  335.6 293.0 %reduce-scatter.5.cloned.1.call-start = ((), (), s32[]{:S(2)}) async-start(), calls=%async_computation.13 | async-start | bytes 10485760 | tf_op jit(solution)/shard_map/reduce_scatter | solution.py:55
  337.2 1.6 copy-start.1
  338.8 1.6 copy-start.2
  338.8 1.6 copy-start.5
Sparse Core Ops, SparseCore 0:
  10.4 30.8 all-gather.17
  43.7 28.0 all-gather.13
  73.7 33.8 all-gather.9
  109.3 43.5 all-gather.19
  154.6 27.1 all-gather.15
  183.6 28.0 all-gather.11
  233.4 28.0 all-gather.21
  263.4 28.0 all-gather.23
  293.4 28.0 all-gather.25
  335.8 144.6 reduce-scatter.2
  483.3 145.2 reduce-scatter.4
where the time goes:
time: 636 us; the launch traced here: 635 us
  waiting for transfers between devices  510 us (80%)
  matrix products  68.4 us (11%)
  local copies, waits for them, and re-layouts  18.1 us (3%)
  between operations  14.6 us (2%)
  blocking collectives  13.3 us (2%)
    reduce_scatter x1, waiting for transfers between devices, on_device(): lax.psum_scatter(grad_out, 'batch', scatter_dimension=1, tiled=True)  145 us
    reduce_scatter x1, waiting for transfers between devices, on_device(): lax.psum_scatter(grad_in, 'batch', scatter_dimension=0, tiled=True)  135 us
    all_gather x3, waiting for transfers between devices, on_device(): lax.all_gather(state.astype(jnp.bfloat16), 'dim', axis=1, tiled=True)  75.2 us
    all_gather x3, waiting for transfers between devices, on_device(): gz_whole = lax.all_gather(gz, 'dim', axis=1, tiled=True)  68.3 us
    all_gather x3, waiting for transfers between devices, on_device(): act_whole = lax.all_gather(act, 'dim', axis=1, tiled=True)  49.5 us
    all_to_all x1, waiting for transfers between devices, on_device(): lax.all_to_all(w_out, 'dim', split_axis=1, concat_axis=0, tiled=True)  33.4 us
    dot_general x3, matrix products, on_device(): term_in = jnp.dot(whole.T, gh, preferred_element_type=jnp.float32)  32.3 us
    dot_general x3, matrix products, on_device(): hidden = jnp.dot(whole, w_in, preferred_element_type=jnp.float32)  14.7 us
  transfers between devices with their start and end apart: 12, of which 11 were waited for; matrix products, arithmetic and copies ran while one was open for 10% of the time, Pallas kernels for 0%

commit v1 on v0

--- a/solution.py
+++ b/solution.py
@@ -22,7 +22,14 @@
         whole = lax.all_gather(state.astype(jnp.bfloat16), "dim", axis=1, tiled=True)
         hidden = jnp.dot(whole, w_in, preferred_element_type=jnp.float32)
         act = jax.nn.silu(hidden).astype(jnp.bfloat16)
-        act_whole = lax.all_gather(act, "dim", axis=1, tiled=True)
+        peers = lax.axis_size("dim")
+        route = [(i, (i + 1) % peers) for i in range(peers)]
+        parts = [act]
+        for far in range(1, peers):
+            parts = [lax.ppermute(parts[0], "dim", route), *parts]
+        full = jnp.concatenate(parts, axis=1)
+        shift = (lax.axis_index("dim") + 1) * parts[-1].shape[1]
+        act_whole = jnp.roll(full, shift, axis=1)
         zval = zscale * jnp.dot(act_whole, out_cols, preferred_element_type=jnp.float32)
         inner = jnp.sum(zval * inc, 1)
         square = jnp.sum(zval * zval, 1)

time: 636 us -> 611 us (0.961)
  waiting for transfers between devices: 510 us -> 482 us
  matrix products: 68.4 us -> 58.6 us
  local copies, waits for them, and re-layouts: 18.1 us -> 27.3 us
    all_gather x3 -> x0, waiting for transfers between devices: 49.5 us -> none  [on_device(): act_whole = lax.all_gather(act, 'dim', axis=1, tiled=True)]
    ppermute x0 -> x21, waiting for transfers between devices: none -> 42.8 us  [on_device(): parts = [lax.ppermute(parts[0], 'dim', route), *parts]]
    all_to_all x1, waiting for transfers between devices: 33.4 us -> 0.01 us  [on_device(): lax.all_to_all(w_out, 'dim', split_axis=1, concat_axis=0, tiled=True)]
    all_gather x3, waiting for transfers between devices: 75.2 us -> 88.4 us  [on_device(): lax.all_gather(state.astype(jnp.bfloat16), 'dim', axis=1, tiled=True)]
    dot_general x3, matrix products: 14.2 us -> 4.99 us  [on_device(): jnp.dot(act_whole, out_cols, preferred_element_type=jnp.float32)]
    unnamed x18 -> x67, local copies, waits for them, and re-layouts: 11.6 us -> 20.7 us
  transfers between devices with their start and end apart: 12 -> 30, of which waited for: 11 -> 24; matrix products, arithmetic and copies ran while one was open for 10% -> 11% of each run, Pallas kernels for 0% -> 0%
where the time goes in v1:
time: 611 us; the launch traced here: 610 us
  waiting for transfers between devices  482 us (79%)
  matrix products  58.6 us (10%)
  local copies, waits for them, and re-layouts  27.3 us (4%)
  between operations  15.3 us (3%)
  blocking collectives  12.8 us (2%)
  starting transfers between devices  8.91 us (1%)
    reduce_scatter x1, waiting for transfers between devices, on_device(): lax.psum_scatter(grad_out, 'batch', scatter_dimension=1, tiled=True)  145 us
    reduce_scatter x1, waiting for transfers between devices, on_device(): lax.psum_scatter(grad_in, 'batch', scatter_dimension=0, tiled=True)  135 us
    all_gather x3, waiting for transfers between devices, on_device(): lax.all_gather(state.astype(jnp.bfloat16), 'dim', axis=1, tiled=True)  88.4 us
    all_gather x3, waiting for transfers between devices, on_device(): gz_whole = lax.all_gather(gz, 'dim', axis=1, tiled=True)  67.3 us
    ppermute x21, waiting for transfers between devices, on_device(): parts = [lax.ppermute(parts[0], 'dim', route), *parts]  42.8 us
    dot_general x3, matrix products, on_device(): term_in = jnp.dot(whole.T, gh, preferred_element_type=jnp.float32)  32.5 us
    unnamed x67, local copies, waits for them, and re-layouts  20.7 us
    dot_general x3, matrix products, on_device(): hidden = jnp.dot(whole, w_in, preferred_element_type=jnp.float32)  13.9 us
  transfers between devices with their start and end apart: 30, of which 24 were waited for; matrix products, arithmetic and copies ran while one was open for 11% of the time, Pallas kernels for 0%

profile of v1, /device:TPU:0, one launch (start us, length us, event | category | flops | bytes accessed | tf_op | source)
XLA Modules:
  0.0 609.9 jit_solution(10079918021536520125)
XLA Ops:
  7.2 2.6 fusion.44
  9.9 0.7 all-gather.9.cloned.1.call-update
  10.7 0.7 all-gather.7.cloned.1.call-update
  11.4 6.5 %copy.14 = bf16[512,4096]{0,1:T(8,128)(2,1)} copy(bf16[512,4096]{1,0:T(8,128)(2,1)} %param.10) | data formatting | bytes 8388608 | tf_op args[3]
  17.9 5.2 all-to-all-start
  23.1 35.1 %all-gather.11.cloned.1.call-done = bf16[256,4096]{1,0:T(8,128)(2,1)} async-done(((bf16[256,512]{1,0:T(8,128)(2,1)}), bf16[256,4096]{1,0:T(8,128)(2,1)}) %all-gather.11.cloned.1.call-update) | async-done | bytes 2097168 | tf_op jit(solution)/shard_map/all_gather | solution.py:22
  58.2 4.1 multiply_convert_fusion
  62.4 0.3 collective-permute-start.14
  62.7 28.3 %all-gather.9.cloned.1.call-done = bf16[256,4096]{1,0:T(8,128)(2,1)} async-done(((bf16[256,512]{1,0:T(8,128)(2,1)}), bf16[256,4096]{1,0:T(8,128)(2,1)}) %all-gather.9.cloned.1.call-update) | async-done | bytes 2097168 | tf_op jit(solution)/shard_map/all_gather | solution.py:22
  90.9 4.9 multiply_convert_fusion.1
  96.1 25.0 %all-gather.7.cloned.1.call-done = bf16[256,4096]{1,0:T(8,128)(2,1)} async-done(((bf16[256,512]{1,0:T(8,128)(2,1)}), bf16[256,4096]{1,0:T(8,128)(2,1)}) %all-gather.7.cloned.1.call-update) | async-done | bytes 2097168 | tf_op jit(solution)/shard_map/all_gather | solution.py:22
  121.1 4.9 multiply_convert_fusion.2
  125.9 0.2 collective-permute-start
  126.2 1.3 collective-permute-start.15
  127.8 4.9 collective-permute-done
  132.6 0.7 copy-done.8
  133.3 2.1 collective-permute-done.15
  135.5 2.8 collective-permute-done.8
  138.3 2.8 collective-permute-done.1
  141.1 2.8 collective-permute-done.16
  143.9 2.8 collective-permute-done.9
  146.7 2.8 collective-permute-done.2
  149.5 2.8 collective-permute-done.17
  152.3 2.8 collective-permute-done.10
  155.1 2.8 collective-permute-done.3
  157.9 2.8 collective-permute-done.18
  160.7 2.9 collective-permute-done.11
  163.7 2.8 collective-permute-done.4
  166.5 2.8 collective-permute-done.19
  170.0 6.5 %copy.15 = bf16[8,512,512]{2,1,0:T(8,128)(2,1)} copy(bf16[8,512,512]{1,2,0:T(8,128)(2,1)} %bitcast.1) | data formatting | bytes 8388608 | tf_op jit(solution)/shard_map/all_to_all | solution.py:19
  176.5 0.7 collective-permute-start.13
  177.3 0.4 collective-permute-done.20
  177.7 1.0 constant_dynamic-update-slice_fusion.23
  178.7 1.0 constant_dynamic-update-slice_fusion.22
  179.7 1.0 constant_dynamic-update-slice_fusion.21
  180.7 1.0 constant_dynamic-update-slice_fusion.20
  181.8 1.6 collective-permute-done.13
  183.5 1.0 constant_dynamic-update-slice_fusion.14
  184.5 1.0 constant_dynamic-update-slice_fusion.13
  185.6 1.3 fusion.2
  187.0 1.3 fusion.5
  188.4 1.2 constant_dynamic-update-slice_fusion.6
  189.6 1.0 constant_dynamic-update-slice_fusion.5
  190.8 2.4 fusion.28
  193.2 12.8 %all-reduce = (f32[256]{0:T(256)S(1)}, f32[256]{0:T(256)S(1)}, f32[256]{0:T(256)S(1)}, f32[256]{0:T(256)S(1)}, f32[256]{0:T(256)S(1)}, /*index=5*/f32[256]{0:T(256)S(1)}, f32[256]{0:T(256)S(1)}) all-reduce(f32[256]{0:T(256)S(1)} %get-tuple-element.14, f32[256]{0:T(256)S(1)} %get-tuple-element.15, ...), channel_id=1, replica_groups=mesh['dim'=8,'batch'=4] {'dim'}, use_global_device_ids=true, to_apply=%region_13.15 | all-reduce | flops 1792 | bytes 14336 | tf_op jit(solution)/shard_map/psum | solution.py:41
  206.0 0.6 broadcast_multiply_fusion
  206.6 2.3 fusion.23
  209.0 0.5 all-gather.15.cloned.1.call-update
  209.6 0.5 all-gather.17.cloned.1.call-update
  210.3 26.0 %all-gather.13.cloned.1.call-done = bf16[256,4096]{1,0:T(8,128)(2,1)} async-done(((bf16[256,512]{1,0:T(8,128)(2,1)}), bf16[256,4096]{1,0:T(8,128)(2,1)}) %all-gather.13.cloned.1.call-update) | async-done | bytes 2097168 | tf_op jit(solution)/shard_map/all_gather | solution.py:52
  236.3 9.6 %fusion.17 = f32[512,4096]{1,0:T(8,128)} fusion(bf16[256,4096]{1,0:T(8,128)(2,1)} %all-gather.7.cloned.1.call-done, bf16[256,4096]{1,0:T(8,128)(2,1)} %all-gather.13.cloned.1.call-done, bf16[512,4096]{1,0:T(8,128)(2,1)} %param.10, f32[256,512]{1,0:T(8,128)} %get-tuple-element.36), kind=kOutput, calls=%fused_computation.25 | convolution fusion | flops 2148663296 | bytes 17301504 | tf_op jit(solution)/shard_map/dot_general | solution.py:57
  245.9 20.2 %all-gather.15.cloned.1.call-done = bf16[256,4096]{1,0:T(8,128)(2,1)} async-done(((bf16[256,512]{1,0:T(8,128)(2,1)}), bf16[256,4096]{1,0:T(8,128)(2,1)}) %all-gather.15.cloned.1.call-update) | async-done | bytes 2097168 | tf_op jit(solution)/shard_map/all_gather | solution.py:52
  266.2 8.8 %fusion.15 = f32[4096,512]{0,1:T(8,128)} fusion(bf16[256,4096]{1,0:T(8,128)(2,1)S(1)} %copy-done.3, bf16[256,4096]{1,0:T(8,128)(2,1)} %all-gather.15.cloned.1.call-done, bf16[512,4096]{1,0:T(8,128)(2,1)} %param.10, f32[256,512]{1,0:T(8,128)} %get-tuple-element.40), kind=kOutput, calls=%fused_computation.23 | convolution fusion | flops 2148663296 | bytes 17301504 | tf_op jit(solution)/shard_map/dot_general | solution.py:57
  274.9 21.1 %all-gather.17.cloned.1.call-done = bf16[256,4096]{1,0:T(8,128)(2,1)} async-done(((bf16[256,512]{1,0:T(8,128)(2,1)}), bf16[256,4096]{1,0:T(8,128)(2,1)}) %all-gather.17.cloned.1.call-update) | async-done | bytes 2097168 | tf_op jit(solution)/shard_map/all_gather | solution.py:52
  296.0 14.1 %fusion = f32[4096,512]{0,1:T(8,128)} fusion(f32[4096,512]{0,1:T(8,128)} %fusion.15, f32[512,4096]{1,0:T(8,128)} %fusion.17, bf16[256,4096]{1,0:T(8,128)(2,1)} %all-gather.11.cloned.1.call-done, bf16[256,4096]{1,0:T(8,128)(2,1)} %all-gather.17.cloned.1.call-done, bf16[512,4096]{1,0:T(8,128)(2,1)} %param.10, f32[256,512]{1,0:T(8,128)S(1)} %get-tuple-element.38), kind=kOutput, calls=%fused_computation.1 | convolution fusion | flops 2152857600 | bytes 34078720 | tf_op jit(solution)/shard_map/dot_general | solution.py:57
  310.2 1.5 copy-done
  311.7 1.3 fusion.55
  313.0 0.3 copy-done.1
  313.3 1.3 fusion.56
  314.6 0.3 copy-done.2
  314.9 4.7 add_add_fusion
  319.6 135.3 %reduce-scatter.3.cloned.1.call-done = f32[1024,512]{0,1:T(8,128)} async-done(((f32[4096,512]{0,1:T(8,128)}), f32[1024,512]{0,1:T(8,128)}) %reduce-scatter.3.cloned.1.call-update) | async-done | bytes 2097168 | tf_op jit(solution)/shard_map/reduce_scatter | solution.py:61
  454.9 2.9 copy.18
  457.8 145.3 %reduce-scatter.5.cloned.1.call-done = f32[512,1024]{1,0:T(8,128)} async-done(((f32[512,4096]{1,0:T(8,128)}), f32[512,1024]{1,0:T(8,128)}) %reduce-scatter.5.cloned.1.call-update) | async-done | bytes 2097168 | tf_op jit(solution)/shard_map/reduce_scatter | solution.py:62
  (91 shorter events, 1.7 us)
Async XLA Ops:
  7.2 51.1 %all-gather.11.cloned.1.call-start = ((), (), s32[]{:S(2)}) async-start(), calls=%async_computation.5 | async-start | bytes 2359296 | tf_op jit(solution)/shard_map/all_gather | solution.py:22
  9.9 81.1 %all-gather.9.cloned.1.call-start = ((), (), s32[]{:S(2)}) async-start(), calls=%async_computation.4 | async-start | bytes 2359296 | tf_op jit(solution)/shard_map/all_gather | solution.py:22
  10.6 110.5 %all-gather.7.cloned.1.call-start = ((), (), s32[]{:S(2)}) async-start(), calls=%async_computation.3 | async-start | bytes 2359296 | tf_op jit(solution)/shard_map/all_gather | solution.py:22
  17.9 152.1 %all-to-all-start = ((bf16[512,8,512]{0,2,1:T(8,128)(2,1)}), bf16[512,8,512]{0,2,1:T(8,128)(2,1)}, u32[]{:S(2)}, u32[]{:S(2)}) async-start(bf16[512,8,512]{0,2,1:T(8,128)(2,1)} %bitcast.83), calls=%async_computation | async-start | bytes 8388608 | tf_op jit(solution)/shard_map/all_to_all | solution.py:19
  23.1 213.2 %all-gather.13.cloned.1.call-start = ((), (), s32[]{:S(2)}) async-start(), calls=%async_computation.6 | async-start | bytes 2359296 | tf_op jit(solution)/shard_map/all_gather | solution.py:52
  62.4 63.8 %collective-permute-start.14 = (bf16[256,512]{1,0:T(8,128)(2,1)S(1)}, bf16[256,512]{1,0:T(8,128)(2,1)S(1)}, u32[]{:S(2)}, u32[]{:S(2)}) collective-permute-start(bf16[256,512]{1,0:T(8,128)(2,1)S(1)} %get-tuple-element.37), channel_id=1, source_target_pairs={{0,4},{4,8},{8,12},{12,16},{16,20},{20,24},{24,28},{28,0},{1,5},{5... | collective-permute-start | bytes 786440 | tf_op jit(solution)/shard_map/ppermute | solution.py:29
  95.8 31.7 %collective-permute-start.7 = (bf16[256,512]{1,0:T(8,128)(2,1)S(1)}, bf16[256,512]{1,0:T(8,128)(2,1)S(1)}, u32[]{:S(2)}, u32[]{:S(2)}) collective-permute-start(bf16[256,512]{1,0:T(8,128)(2,1)S(1)} %get-tuple-element.39), channel_id=1, source_target_pairs={{0,4},{4,8},{8,12},{12,16},{16,20},{20,24},{24,28},{28,0},{1,5},{5... | collective-permute-start | bytes 786440 | tf_op jit(solution)/shard_map/ppermute | solution.py:29
  125.9 6.7 %collective-permute-start = (bf16[256,512]{1,0:T(8,128)(2,1)S(1)}, bf16[256,512]{1,0:T(8,128)(2,1)S(1)}, u32[]{:S(2)}, u32[]{:S(2)}) collective-permute-start(bf16[256,512]{1,0:T(8,128)(2,1)S(1)} %get-tuple-element.35), channel_id=1, source_target_pairs={{0,4},{4,8},{8,12},{12,16},{16,20},{20,24},{24,28},{28,0},{1,5},{5... | collective-permute-start | bytes 786440 | tf_op jit(solution)/shard_map/ppermute | solution.py:29
  126.2 9.3 %collective-permute-start.15 = (bf16[256,512]{1,0:T(8,128)(2,1)S(1)}, bf16[256,512]{1,0:T(8,128)(2,1)S(1)}, u32[]{:S(2)}, u32[]{:S(2)}) collective-permute-start(bf16[256,512]{1,0:T(8,128)(2,1)S(1)} %collective-permute-done.14), channel_id=1, source_target_pairs={{0,4},{4,8},{8,12},{12,16},{16,20},{20,24},{24,28},{28,0},{1,5},{5... | collective-permute-start | bytes 786440 | tf_op jit(solution)/shard_map/ppermute | solution.py:29
  127.5 10.7 %collective-permute-start.8 = (bf16[256,512]{1,0:T(8,128)(2,1)S(1)}, bf16[256,512]{1,0:T(8,128)(2,1)S(1)}, u32[]{:S(2)}, u32[]{:S(2)}) collective-permute-start(bf16[256,512]{1,0:T(8,128)(2,1)S(1)} %collective-permute-done.7), channel_id=1, source_target_pairs={{0,4},{4,8},{8,12},{12,16},{16,20},{20,24},{24,28},{28,0},{1,5},{5... | collective-permute-start | bytes 786440 | tf_op jit(solution)/shard_map/ppermute | solution.py:29
  132.6 0.7 copy-start.8
  133.3 7.7 %collective-permute-start.1 = (bf16[256,512]{1,0:T(8,128)(2,1)S(1)}, bf16[256,512]{1,0:T(8,128)(2,1)S(1)}, u32[]{:S(2)}, u32[]{:S(2)}) collective-permute-start(bf16[256,512]{1,0:T(8,128)(2,1)S(1)} %collective-permute-done), channel_id=1, source_target_pairs={{0,4},{4,8},{8,12},{12,16},{16,20},{20,24},{24,28},{28,0},{1,5},{5... | collective-permute-start | bytes 786440 | tf_op jit(solution)/shard_map/ppermute | solution.py:29
  135.5 8.4 %collective-permute-start.16 = (bf16[256,512]{1,0:T(8,128)(2,1)S(1)}, bf16[256,512]{1,0:T(8,128)(2,1)S(1)}, u32[]{:S(2)}, u32[]{:S(2)}) collective-permute-start(bf16[256,512]{1,0:T(8,128)(2,1)S(1)} %collective-permute-done.15), channel_id=1, source_target_pairs={{0,4},{4,8},{8,12},{12,16},{16,20},{20,24},{24,28},{28,0},{1,5},{5... | collective-permute-start | bytes 786440 | tf_op jit(solution)/shard_map/ppermute | solution.py:29
  138.3 8.4 %collective-permute-start.9 = (bf16[256,512]{1,0:T(8,128)(2,1)S(1)}, bf16[256,512]{1,0:T(8,128)(2,1)S(1)}, u32[]{:S(2)}, u32[]{:S(2)}) collective-permute-start(bf16[256,512]{1,0:T(8,128)(2,1)S(1)} %collective-permute-done.8), channel_id=1, source_target_pairs={{0,4},{4,8},{8,12},{12,16},{16,20},{20,24},{24,28},{28,0},{1,5},{5... | collective-permute-start | bytes 786440 | tf_op jit(solution)/shard_map/ppermute | solution.py:29
  141.1 35.4 %copy-start.10 = (bf16[256,512]{1,0:T(8,128)(2,1)}, bf16[256,512]{1,0:T(8,128)(2,1)S(1)}, u32[]{:S(2)}) copy-start(bf16[256,512]{1,0:T(8,128)(2,1)S(1)} %collective-permute-done.1) | copy-start | bytes 786436
  141.1 8.4 %collective-permute-start.2 = (bf16[256,512]{1,0:T(8,128)(2,1)S(1)}, bf16[256,512]{1,0:T(8,128)(2,1)S(1)}, u32[]{:S(2)}, u32[]{:S(2)}) collective-permute-start(bf16[256,512]{1,0:T(8,128)(2,1)S(1)} %collective-permute-done.1), channel_id=1, source_target_pairs={{0,4},{4,8},{8,12},{12,16},{16,20},{20,24},{24,28},{28,0},{1,5},{5... | collective-permute-start | bytes 786440 | tf_op jit(solution)/shard_map/ppermute | solution.py:29
  143.9 22.6 %copy-start.16 = (bf16[256,512]{1,0:T(8,128)(2,1)}, bf16[256,512]{1,0:T(8,128)(2,1)S(1)}, u32[]{:S(2)}) copy-start(bf16[256,512]{1,0:T(8,128)(2,1)S(1)} %collective-permute-done.16) | copy-start | bytes 786436
  143.9 8.4 %collective-permute-start.17 = (bf16[256,512]{1,0:T(8,128)(2,1)S(1)}, bf16[256,512]{1,0:T(8,128)(2,1)S(1)}, u32[]{:S(2)}, u32[]{:S(2)}) collective-permute-start(bf16[256,512]{1,0:T(8,128)(2,1)S(1)} %collective-permute-done.16), channel_id=1, source_target_pairs={{0,4},{4,8},{8,12},{12,16},{16,20},{20,24},{24,28},{28,0},{1,5},{5... | collective-permute-start | bytes 786440 | tf_op jit(solution)/shard_map/ppermute | solution.py:29
  146.7 8.4 %collective-permute-start.10 = (bf16[256,512]{1,0:T(8,128)(2,1)S(1)}, bf16[256,512]{1,0:T(8,128)(2,1)S(1)}, u32[]{:S(2)}, u32[]{:S(2)}) collective-permute-start(bf16[256,512]{1,0:T(8,128)(2,1)S(1)} %collective-permute-done.9), channel_id=1, source_target_pairs={{0,4},{4,8},{8,12},{12,16},{16,20},{20,24},{24,28},{28,0},{1,5},{5... | collective-permute-start | bytes 786440 | tf_op jit(solution)/shard_map/ppermute | solution.py:29
  149.5 27.0 %copy-start.12 = (bf16[256,512]{1,0:T(8,128)(2,1)}, bf16[256,512]{1,0:T(8,128)(2,1)S(1)}, u32[]{:S(2)}) copy-start(bf16[256,512]{1,0:T(8,128)(2,1)S(1)} %collective-permute-done.2) | copy-start | bytes 786436
  149.5 8.4 %collective-permute-start.3 = (bf16[256,512]{1,0:T(8,128)(2,1)S(1)}, bf16[256,512]{1,0:T(8,128)(2,1)S(1)}, u32[]{:S(2)}, u32[]{:S(2)}) collective-permute-start(bf16[256,512]{1,0:T(8,128)(2,1)S(1)} %collective-permute-done.2), channel_id=1, source_target_pairs={{0,4},{4,8},{8,12},{12,16},{16,20},{20,24},{24,28},{28,0},{1,5},{5... | collective-permute-start | bytes 786440 | tf_op jit(solution)/shard_map/ppermute | solution.py:29
  152.3 17.0 %copy-start.20 = (bf16[256,512]{1,0:T(8,128)(2,1)}, bf16[256,512]{1,0:T(8,128)(2,1)S(1)}, u32[]{:S(2)}) copy-start(bf16[256,512]{1,0:T(8,128)(2,1)S(1)} %collective-permute-done.17) | copy-start | bytes 786436
  152.3 8.4 %collective-permute-start.18 = (bf16[256,512]{1,0:T(8,128)(2,1)S(1)}, bf16[256,512]{1,0:T(8,128)(2,1)S(1)}, u32[]{:S(2)}, u32[]{:S(2)}) collective-permute-start(bf16[256,512]{1,0:T(8,128)(2,1)S(1)} %collective-permute-done.17), channel_id=1, source_target_pairs={{0,4},{4,8},{8,12},{12,16},{16,20},{20,24},{24,28},{28,0},{1,5},{5... | collective-permute-start | bytes 786440 | tf_op jit(solution)/shard_map/ppermute | solution.py:29
  155.1 11.3 %copy-start.18 = (bf16[256,512]{1,0:T(8,128)(2,1)}, bf16[256,512]{1,0:T(8,128)(2,1)S(1)}, u32[]{:S(2)}) copy-start(bf16[256,512]{1,0:T(8,128)(2,1)S(1)} %collective-permute-done.10) | copy-start | bytes 786436
  155.1 8.5 %collective-permute-start.11 = (bf16[256,512]{1,0:T(8,128)(2,1)S(1)}, bf16[256,512]{1,0:T(8,128)(2,1)}, u32[]{:S(2)}, u32[]{:S(2)}) collective-permute-start(bf16[256,512]{1,0:T(8,128)(2,1)S(1)} %collective-permute-done.10), channel_id=1, source_target_pairs={{0,4},{4,8},{8,12},{12,16},{16,20},{20,24},{24,28},{28,0},{1,5},{5... | collective-permute-start | bytes 786440 | tf_op jit(solution)/shard_map/ppermute | solution.py:29
  157.9 18.5 %copy-start.14 = (bf16[256,512]{1,0:T(8,128)(2,1)}, bf16[256,512]{1,0:T(8,128)(2,1)S(1)}, u32[]{:S(2)}) copy-start(bf16[256,512]{1,0:T(8,128)(2,1)S(1)} %collective-permute-done.3) | copy-start | bytes 786436
  157.9 8.5 %collective-permute-start.4 = (bf16[256,512]{1,0:T(8,128)(2,1)S(1)}, bf16[256,512]{1,0:T(8,128)(2,1)}, u32[]{:S(2)}, u32[]{:S(2)}) collective-permute-start(bf16[256,512]{1,0:T(8,128)(2,1)S(1)} %collective-permute-done.3), channel_id=1, source_target_pairs={{0,4},{4,8},{8,12},{12,16},{16,20},{20,24},{24,28},{28,0},{1,5},{5... | collective-permute-start | bytes 786440 | tf_op jit(solution)/shard_map/ppermute | solution.py:29
  160.7 8.5 %copy-start.21 = (bf16[256,512]{1,0:T(8,128)(2,1)}, bf16[256,512]{1,0:T(8,128)(2,1)S(1)}, u32[]{:S(2)}) copy-start(bf16[256,512]{1,0:T(8,128)(2,1)S(1)} %collective-permute-done.18) | copy-start | bytes 786436
  160.7 8.5 %collective-permute-start.19 = (bf16[256,512]{1,0:T(8,128)(2,1)S(1)}, bf16[256,512]{1,0:T(8,128)(2,1)}, u32[]{:S(2)}, u32[]{:S(2)}) collective-permute-start(bf16[256,512]{1,0:T(8,128)(2,1)S(1)} %collective-permute-done.18), channel_id=1, source_target_pairs={{0,4},{4,8},{8,12},{12,16},{16,20},{20,24},{24,28},{28,0},{1,5},{5... | collective-permute-start | bytes 786440 | tf_op jit(solution)/shard_map/ppermute | solution.py:29
  163.6 12.8 %collective-permute-start.12 = (bf16[256,512]{1,0:T(8,128)(2,1)}, bf16[256,512]{1,0:T(8,128)(2,1)}, u32[]{:S(2)}, u32[]{:S(2)}) collective-permute-start(bf16[256,512]{1,0:T(8,128)(2,1)} %collective-permute-done.11), channel_id=1, source_target_pairs={{0,4},{4,8},{8,12},{12,16},{16,20},{20,24},{24,28},{28,0},{1,5},{5... | collective-permute-start | bytes 786440 | tf_op jit(solution)/shard_map/ppermute | solution.py:29
  166.5 10.7 %collective-permute-start.5 = (bf16[256,512]{1,0:T(8,128)(2,1)}, bf16[256,512]{1,0:T(8,128)(2,1)}, u32[]{:S(2)}, u32[]{:S(2)}) collective-permute-start(bf16[256,512]{1,0:T(8,128)(2,1)} %collective-permute-done.4), channel_id=1, source_target_pairs={{0,4},{4,8},{8,12},{12,16},{16,20},{20,24},{24,28},{28,0},{1,5},{5... | collective-permute-start | bytes 786440 | tf_op jit(solution)/shard_map/ppermute | solution.py:29
  169.3 8.4 %collective-permute-start.20 = (bf16[256,512]{1,0:T(8,128)(2,1)}, bf16[256,512]{1,0:T(8,128)(2,1)}, u32[]{:S(2)}, u32[]{:S(2)}) collective-permute-start(bf16[256,512]{1,0:T(8,128)(2,1)} %collective-permute-done.19), channel_id=1, source_target_pairs={{0,4},{4,8},{8,12},{12,16},{16,20},{20,24},{24,28},{28,0},{1,5},{5... | collective-permute-start | bytes 786440 | tf_op jit(solution)/shard_map/ppermute | solution.py:29
  176.5 5.2 copy-start.17
  176.5 7.0 %collective-permute-start.13 = (bf16[256,512]{1,0:T(8,128)(2,1)}, bf16[256,512]{1,0:T(8,128)(2,1)S(1)}, u32[]{:S(2)}, u32[]{:S(2)}) collective-permute-start(bf16[256,512]{1,0:T(8,128)(2,1)} %collective-permute-done.12), channel_id=1, source_target_pairs={{0,4},{4,8},{8,12},{12,16},{16,20},{20,24},{24,28},{28,0},{1,5},{5... | collective-permute-start | bytes 786440 | tf_op jit(solution)/shard_map/ppermute | solution.py:29
  177.2 11.1 %collective-permute-start.6 = (bf16[256,512]{1,0:T(8,128)(2,1)}, bf16[256,512]{1,0:T(8,128)(2,1)S(1)}, u32[]{:S(2)}, u32[]{:S(2)}) collective-permute-start(bf16[256,512]{1,0:T(8,128)(2,1)} %collective-permute-done.5), channel_id=1, source_target_pairs={{0,4},{4,8},{8,12},{12,16},{16,20},{20,24},{24,28},{28,0},{1,5},{5... | collective-permute-start | bytes 786440 | tf_op jit(solution)/shard_map/ppermute | solution.py:29
  180.6 4.8 copy-start.19
  181.8 3.8 copy-start.5
  186.9 3.6 copy-start.15
  187.0 3.6 copy-start.13
  187.0 3.7 copy-start.11
  188.3 2.5 copy-start.6
  188.3 2.4 copy-start.9
  188.3 2.5 copy-start.4
  188.3 2.5 copy-start.7
  208.9 57.2 %all-gather.15.cloned.1.call-start = ((), (), s32[]{:S(2)}) async-start(), calls=%async_computation.7 | async-start | bytes 2359296 | tf_op jit(solution)/shard_map/all_gather | solution.py:52
  209.5 86.5 %all-gather.17.cloned.1.call-start = ((), (), s32[]{:S(2)}) async-start(), calls=%async_computation.8 | async-start | bytes 2359296 | tf_op jit(solution)/shard_map/all_gather | solution.py:52
  210.1 244.8 %reduce-scatter.3.cloned.1.call-start = ((), (), s32[]{:S(2)}) async-start(), calls=%async_computation.9 | async-start | bytes 10485760 | tf_op jit(solution)/shard_map/reduce_scatter | solution.py:61
  236.3 29.9 %copy-start.3 = (bf16[256,4096]{1,0:T(8,128)(2,1)S(1)}, bf16[256,4096]{1,0:T(8,128)(2,1)}, u32[]{:S(2)}) copy-start(bf16[256,4096]{1,0:T(8,128)(2,1)} %all-gather.9.cloned.1.call-done) | copy-start | bytes 6291460
  310.1 1.6 copy-start
  310.1 293.0 %reduce-scatter.5.cloned.1.call-start = ((), (), s32[]{:S(2)}) async-start(), calls=%async_computation.10 | async-start | bytes 10485760 | tf_op jit(solution)/shard_map/reduce_scatter | solution.py:62
  311.7 1.6 copy-start.1
  313.3 1.6 copy-start.2
Sparse Core Ops, SparseCore 0:
  10.4 47.7 all-gather.10
  60.7 30.2 all-gather.8
  92.8 28.2 all-gather.6
  209.0 27.1 all-gather.12
  238.0 28.0 all-gather.14
  267.9 28.0 all-gather.16
  310.3 144.6 reduce-scatter.2
  457.8 145.2 reduce-scatter.4
